TPU v7x, 32 devices: a whole 2x2x4 slice. The times are simulated.
32 devices in a mesh: dp: 16 (over z, y, x), seq: 2 (over core).
Axes of the slice: x: 2, y: 2, z: 4, core: 2. Of those that a mesh axis runs over, the one named last changes fastest.
Arguments:
- patches: bfloat16 [32, 256, 768], P('dp', 'seq'), may hold values from -6 to 6
- block_masks: int32 [32, 196], P('dp'), may hold values from 0 to 1, as said below
- split_rows: int32 [32], P('dp'), may hold values from 6 to 8, as said below
- span_order: int32 [2720], replicated, may hold values from 0 to 2719, as said below
- weights: float32 [10880, 768], P('dp')
- teacher: bfloat16 [10880, 768], P('dp')
- first_moment: float32 [10880, 768], P('dp')
- second_moment: float32 [10880, 768], P('dp')
- step_count: int32 [1], replicated, may hold values from 2 to 20
Outputs:
- total_loss: float32 [], replicated
- grad_norm: float32 [], replicated
- updated_weights: float32 [10880, 768], P('dp')
- weights_copy: bfloat16 [10880, 768], P('dp')
- updated_first: float32 [10880, 768], P('dp')
- updated_second: float32 [10880, 768], P('dp')
Inputs may be any that keep to these rules, and one draw needn't show every extreme that they name: `block_masks`: cells are row-major over the 14 x 14 grid; masks come in aligned 2 x 2 blocks of cells. Rows 0 to split_rows - 1 of an image lie on seq index 0 after its CLS slot, the rest on seq index 1 from slot 0. `span_order`: each of 0 to 2719 once.
All inputs are finite; a program needn't handle non-finite values.
Results may differ from a plain program's by a relative error of at most 0.001.
The roundings to bfloat16 on the way count: a program that leaves them out, or rounds other values in their place, can miss the bound.
Values may be sent and summed in bfloat16 or wider, within the bound.
A program may use at most 256 MiB of HBM per device.

v0:
```python
import math
import jax
import jax.numpy as jnp
from jax import lax
from jax.sharding import PartitionSpec as P

D = 768
HEADS = 12
HD = 64
FF = 3072
PP = 768
GRID = 14
SL = 128
CR = 4
BETA = 2.0
CLIP = 0.01
LEARN = 0.03
DECAY = 0.05
BETA_ONE = 0.9
BETA_TWO = 0.999
ADAM_EPS = 1e-08
NORM_EPS = 1e-06


def from_partner(shard, axis, bit):
    return lax.ppermute(shard, axis, [(i, i ^ 1 << bit) for i in range(lax.axis_size(axis))])


def layout():
    return [
        ("cls", 1, (D,)),
        ("mask_tok", 1, (D,)),
        ("b_pe", 1, (D,)),
        ("ln1_g", 1, (D,)),
        ("ln1_b", 1, (D,)),
        ("b_out", 1, (D,)),
        ("ln2_g", 1, (D,)),
        ("ln2_b", 1, (D,)),
        ("b_two", 1, (D,)),
        ("lnf_g", 1, (D,)),
        ("lnf_b", 1, (D,)),
        ("b_head", 1, (D,)),
        ("b_one", FF // D, (FF,)),
        ("w_pe", PP, (PP, D)),
        ("w_qkv", 3 * D, (D, 3 * D)),
        ("w_out", D, (D, D)),
        ("w_one", FF, (D, FF)),
        ("w_two", FF, (FF, D)),
        ("w_head", D, (D, D)),
    ]


def unpack(flat):
    tables = {}
    offset = 0
    for entry_name, entry_rows, entry_shape in layout():
        tables[entry_name] = flat[offset : offset + entry_rows].reshape(entry_shape)
        offset = offset + entry_rows
    return tables


def pack_flat(tables, total_rows):
    pieces = [tables[entry_name].reshape(-1, D) for entry_name, entry_rows, entry_shape in layout()]
    stacked = jnp.concatenate(pieces, 0)
    return jnp.concatenate(
        [stacked, jnp.zeros((total_rows - stacked.shape[0], D), stacked.dtype)], 0
    )


def reorder(stored, order):
    return stored.reshape(order.shape[0], -1, D)[order].reshape(-1, D)


def slot_info(split_rows, seq_side):
    column = jnp.arange(SL)[None, :]
    split_col = split_rows[:, None]
    first_side = seq_side == 0
    first_slot = jnp.where(first_side, 1, 0)
    filled = jnp.where(first_side, split_col * GRID, (GRID - split_col) * GRID)
    offset = jnp.where(first_side, -1, split_col * GRID)
    is_patch = (column >= first_slot) & (column < first_slot + filled)
    is_cls = first_side & (column == 0) & (split_col >= 0)
    grid_cell = jnp.clip(column + offset, 0, GRID * GRID - 1)
    return (is_patch, is_cls, grid_cell)


def sincos(grid_cell):
    quarter = D // 4
    frequency = 1.0 / 10000.0 ** (jnp.arange(quarter).astype(jnp.float32) / quarter)
    rows_at = (grid_cell // GRID).astype(jnp.float32)[..., None] * frequency
    cols_at = (grid_cell % GRID).astype(jnp.float32)[..., None] * frequency
    return jnp.concatenate(
        [jnp.sin(rows_at), jnp.cos(rows_at), jnp.sin(cols_at), jnp.cos(cols_at)], -1
    )


def layer_norm(values):
    center = jnp.mean(values, -1, keepdims=True)
    centred = values - center
    return centred * lax.rsqrt(jnp.mean(centred * centred, -1, keepdims=True) + NORM_EPS)


def matmul_f32(left_mat, right_mat):
    return jnp.dot(left_mat, right_mat, preferred_element_type=jnp.float32)


def weight_grad(left_mat, right_mat):
    return lax.dot_general(
        left_mat, right_mat, (((0,), (0,)), ((), ())), preferred_element_type=jnp.float32
    )


def back_dot(left_mat, right_mat):
    return lax.dot_general(
        left_mat, right_mat, (((1,), (1,)), ((), ())), preferred_element_type=jnp.float32
    )


def vector(params, entry_name):
    return params[entry_name].astype(jnp.float32)


def column_sums(values):
    return jnp.sum(values.astype(jnp.float32), 0)


def norm_fwd(values, gain_vec, bias_vec):
    center = jnp.mean(values, -1, keepdims=True)
    centred = values - center
    inverse = lax.rsqrt(jnp.mean(centred * centred, -1, keepdims=True) + NORM_EPS)
    normed = centred * inverse
    return (normed * gain_vec + bias_vec, normed, inverse)


def norm_back(grad_out, normed, inverse, gain_vec):
    scaled = grad_out * gain_vec
    grad_in = inverse * (
        scaled
        - jnp.mean(scaled, -1, keepdims=True)
        - normed * jnp.mean(scaled * normed, -1, keepdims=True)
    )
    return (grad_in, jnp.sum(grad_out * normed, 0), jnp.sum(grad_out, 0))


def place_tokens(params, embedded, is_patch, is_cls, hidden_mask, position):
    on_grid = embedded.reshape(is_patch.shape + (D,)) + position
    tokens = jnp.where(is_patch[..., None], on_grid, 0.0)
    tokens = jnp.where(hidden_mask[..., None], vector(params, "mask_tok") + position, tokens)
    tokens = jnp.where(is_cls[..., None], vector(params, "cls"), tokens)
    return tokens.reshape(-1, D)


def project(params, tokens, length):
    normed_in, normed, inverse = norm_fwd(tokens, vector(params, "ln1_g"), vector(params, "ln1_b"))
    normed_in = normed_in.astype(jnp.bfloat16)
    packed = (
        matmul_f32(normed_in, params["w_qkv"])
        .astype(jnp.bfloat16)
        .reshape(-1, length, 3, HEADS, HD)
    )
    return (normed_in, normed, inverse, packed[:, :, 0], packed[:, :, 1], packed[:, :, 2])


def scores_of(queries, keys_block, key_live):
    raw_scores = jnp.einsum(
        "bqhd,bkhd->bhqk", queries, keys_block, preferred_element_type=jnp.float32
    ) * HD ** (-0.5)
    return jnp.where(key_live[:, None, None, :], raw_scores, -1e30)


def attend(queries, blocks):
    scores = [scores_of(queries, block[0], block[2]) for block in blocks]
    highest = reduce_max([jnp.max(member, -1, keepdims=True) for member in scores])
    summed = sum([jnp.sum(jnp.exp(member - highest), -1, keepdims=True) for member in scores])
    logsum = highest + jnp.log(summed)
    mixed_out = sum(
        [
            jnp.einsum(
                "bhqk,bkhd->bqhd",
                jnp.exp(member - logsum).astype(jnp.bfloat16),
                block[1],
                preferred_element_type=jnp.float32,
            )
            for member, block in zip(scores, blocks)
        ]
    )
    return (mixed_out.astype(jnp.bfloat16).reshape(-1, D), logsum)


def reduce_max(members):
    highest = members[0]
    for member in members[1:]:
        highest = jnp.maximum(highest, member)
    return highest


def finish(params, tokens, queries, blocks):
    mixed_out, logsum = attend(queries, blocks)
    hidden = tokens + matmul_f32(mixed_out, params["w_out"]) + vector(params, "b_out")
    normed_two_in, normed_two, inverse_two = norm_fwd(
        hidden, vector(params, "ln2_g"), vector(params, "ln2_b")
    )
    normed_two_in = normed_two_in.astype(jnp.bfloat16)
    upward = matmul_f32(normed_two_in, params["w_one"]) + vector(params, "b_one")
    gelled = jax.nn.gelu(upward).astype(jnp.bfloat16)
    output = hidden + matmul_f32(gelled, params["w_two"]) + vector(params, "b_two")
    return (output, (mixed_out, logsum, normed_two, inverse_two, normed_two_in, upward, gelled))


def layer_back(params, grad_out, saved, far_blocks, key_live, gradients):
    (
        normed_in,
        normed,
        inverse,
        queries,
        keys_loc,
        values_loc,
        mixed_out,
        logsum,
        normed_two,
        inverse_two,
        normed_two_in,
        upward,
        gelled,
    ) = saved
    length = queries.shape[1]
    blocks = [(keys_loc, values_loc, key_live)] + far_blocks
    grad_branch = grad_out.astype(jnp.bfloat16)
    gradients["w_two"] = weight_grad(gelled, grad_branch)
    gradients["b_two"] = column_sums(grad_branch)
    unused, gelu_pull = jax.vjp(jax.nn.gelu, upward)
    grad_up = gelu_pull(back_dot(grad_branch, params["w_two"]))[0].astype(jnp.bfloat16)
    gradients["w_one"] = weight_grad(normed_two_in, grad_up)
    gradients["b_one"] = column_sums(grad_up)
    grad_two, gradients["ln2_g"], gradients["ln2_b"] = norm_back(
        back_dot(grad_up, params["w_one"]), normed_two, inverse_two, vector(params, "ln2_g")
    )
    grad_hidden = grad_out + grad_two
    grad_attn = grad_hidden.astype(jnp.bfloat16)
    gradients["w_out"] = weight_grad(mixed_out, grad_attn)
    gradients["b_out"] = column_sums(grad_attn)
    grad_mixed = (
        back_dot(grad_attn, params["w_out"]).astype(jnp.bfloat16).reshape(-1, length, HEADS, HD)
    )
    probs = [jnp.exp(scores_of(queries, block[0], block[2]) - logsum) for block in blocks]
    pushes = [
        jnp.einsum("bqhd,bkhd->bhqk", grad_mixed, block[1], preferred_element_type=jnp.float32)
        for block in blocks
    ]
    common = sum([jnp.sum(prob * push, -1, keepdims=True) for prob, push in zip(probs, pushes)])
    grad_scores = [
        (prob * (push - common)).astype(jnp.bfloat16) for prob, push in zip(probs, pushes)
    ]
    key_scale = HD ** (-0.5)
    grad_queries = (
        sum(
            [
                jnp.einsum("bhqk,bkhd->bqhd", member, block[0], preferred_element_type=jnp.float32)
                for member, block in zip(grad_scores, blocks)
            ]
        )
        * key_scale
    )
    key_grads = [
        jnp.einsum("bhqk,bqhd->bkhd", member, queries, preferred_element_type=jnp.float32)
        * key_scale
        for member in grad_scores
    ]
    value_grads = [
        jnp.einsum(
            "bhqk,bqhd->bkhd",
            prob.astype(jnp.bfloat16),
            grad_mixed,
            preferred_element_type=jnp.float32,
        )
        for prob in probs
    ]
    grad_keys, grad_values = (key_grads[0], value_grads[0])
    returned = from_partner(
        jnp.stack([key_grads[1], value_grads[1]]).astype(jnp.bfloat16), "seq", 0
    ).astype(jnp.float32)
    grad_keys = grad_keys + returned[0]
    grad_values = grad_values + returned[1]
    grad_packed = (
        jnp.stack([grad_queries, grad_keys, grad_values], 2).astype(jnp.bfloat16).reshape(-1, 3 * D)
    )
    gradients["w_qkv"] = weight_grad(normed_in, grad_packed)
    grad_first, gradients["ln1_g"], gradients["ln1_b"] = norm_back(
        back_dot(grad_packed, params["w_qkv"]), normed, inverse, vector(params, "ln1_g")
    )
    return grad_hidden + grad_first


def on_device(
    patches,
    block_masks,
    split_rows,
    span_order,
    weights,
    teacher,
    first_moment,
    second_moment,
    step_count,
):
    gathered, teacher_all = (
        lax.all_gather(weights.astype(jnp.bfloat16), "dp", axis=0, tiled=True),
        lax.all_gather(teacher, "dp", axis=0, tiled=True),
    )
    inverse_order = jnp.argsort(span_order)
    params = unpack(reorder(gathered, inverse_order))
    teacher_params = unpack(reorder(teacher_all, inverse_order))
    seq_side = lax.axis_index("seq")
    is_patch, is_cls, grid_cell = slot_info(split_rows, seq_side)
    far_patch, far_cls, far_cell = slot_info(split_rows, 1 - seq_side)
    far_live = far_patch | far_cls
    length = SL
    images = patches.shape[0]
    hidden_mask = (jnp.take_along_axis(block_masks, grid_cell, 1) == 1) & is_patch
    key_live = is_patch | is_cls
    masked_count = lax.psum(jnp.sum(hidden_mask.astype(jnp.float32)), ("dp", "seq"))
    position = sincos(grid_cell)
    pixels = patches.reshape(-1, PP)
    embedded_teacher = matmul_f32(pixels, teacher_params["w_pe"]) + vector(teacher_params, "b_pe")
    embedded_student = matmul_f32(pixels, params["w_pe"]) + vector(params, "b_pe")
    tokens_teacher = place_tokens(
        teacher_params, embedded_teacher, is_patch, is_cls, jnp.zeros_like(hidden_mask), position
    )
    tokens_student = place_tokens(params, embedded_student, is_patch, is_cls, hidden_mask, position)
    teacher_proj = project(teacher_params, tokens_teacher, length)
    student_proj = project(params, tokens_student, length)
    arrived = from_partner(
        jnp.stack([teacher_proj[4], teacher_proj[5], student_proj[4], student_proj[5]]), "seq", 0
    )
    teacher_far = [(arrived[0], arrived[1], far_live)]
    student_far = [(arrived[2], arrived[3], far_live)]
    teacher_out, unused = finish(
        teacher_params,
        tokens_teacher,
        teacher_proj[3],
        [(teacher_proj[4], teacher_proj[5], key_live)] + teacher_far,
    )
    target = layer_norm(teacher_out)
    student_out, finish_saved = finish(
        params,
        tokens_student,
        student_proj[3],
        [(student_proj[4], student_proj[5], key_live)] + student_far,
    )
    final_in, final_normed, final_inverse = norm_fwd(
        student_out, vector(params, "lnf_g"), vector(params, "lnf_b")
    )
    final_in = final_in.astype(jnp.bfloat16)
    predicted = matmul_f32(final_in, params["w_head"]) + vector(params, "b_head")
    difference = predicted - target
    magnitude = jnp.abs(difference)
    elementwise = jnp.where(
        magnitude < BETA, 0.5 * difference * difference / BETA, magnitude - 0.5 * BETA
    )
    selected = hidden_mask.reshape(-1)[:, None]
    loss_scale = 1.0 / (math.sqrt(D) * masked_count)
    total_loss = lax.psum(
        jnp.sum(jnp.where(selected, elementwise, 0.0)) * loss_scale, ("dp", "seq")
    )
    grad_pred = (
        jnp.where(selected, jnp.clip(difference / BETA, -1.0, 1.0), 0.0) * loss_scale
    ).astype(jnp.bfloat16)
    gradients = {}
    gradients["w_head"] = weight_grad(final_in, grad_pred)
    gradients["b_head"] = column_sums(grad_pred)
    grad_tokens, gradients["lnf_g"], gradients["lnf_b"] = norm_back(
        back_dot(grad_pred, params["w_head"]), final_normed, final_inverse, vector(params, "lnf_g")
    )
    saved = tuple(student_proj) + tuple(finish_saved)
    grad_tokens = layer_back(params, grad_tokens, saved, student_far, key_live, gradients)
    grad_slots = grad_tokens.reshape(images, length, D)
    visible = (is_patch & jnp.logical_not(hidden_mask))[..., None]
    grad_embed = jnp.where(visible, grad_slots, 0.0).astype(jnp.bfloat16).reshape(-1, D)
    gradients["w_pe"] = weight_grad(pixels, grad_embed)
    gradients["b_pe"] = column_sums(grad_embed)
    gradients["mask_tok"] = jnp.sum(jnp.where(hidden_mask[..., None], grad_slots, 0.0), (0, 1))
    gradients["cls"] = jnp.sum(jnp.where(is_cls[..., None], grad_slots, 0.0), (0, 1))
    stored_grad = reorder(pack_flat(gradients, span_order.shape[0] * CR), span_order)
    owned_grad = lax.psum_scatter(stored_grad, "dp", scatter_dimension=0, tiled=True)
    owned_grad = lax.psum(owned_grad, "seq")
    squares = lax.psum(jnp.sum(owned_grad * owned_grad), "dp")
    grad_norm = jnp.sqrt(squares)
    clipped = owned_grad * (CLIP / jnp.maximum(grad_norm, CLIP))
    updated_first = BETA_ONE * first_moment + (1.0 - BETA_ONE) * clipped
    updated_second = BETA_TWO * second_moment + (1.0 - BETA_TWO) * clipped * clipped
    steps_done = step_count[0].astype(jnp.float32)
    adam_step = (
        updated_first
        / (1.0 - BETA_ONE**steps_done)
        / (jnp.sqrt(updated_second / (1.0 - BETA_TWO**steps_done)) + ADAM_EPS)
    )
    updated_weights = weights - LEARN * (adam_step + DECAY * weights)
    return (
        total_loss,
        grad_norm,
        updated_weights,
        updated_weights.astype(jnp.bfloat16),
        updated_first,
        updated_second,
    )


def solution(mesh):
    placed = (
        P("dp", "seq", None),
        P("dp", None),
        P("dp"),
        P(),
        P("dp", None),
        P("dp", None),
        P("dp", None),
        P("dp", None),
        P(),
    )
    return jax.shard_map(
        on_device,
        mesh=mesh,
        in_specs=placed,
        out_specs=(P(), P(), P("dp", None), P("dp", None), P("dp", None), P("dp", None)),
        check_vma=False,
    )
```

profile of v0, /device:TPU:0, one launch (start us, length us, event | category | flops | bytes accessed | tf_op | source)
XLA Modules:
  0.0 1527.9 jit_solution(8221068962807406303)
XLA Ops:
  8.0 2.7 convert_element_type.232
  10.8 2.5 gather_fusion.3
  14.6 44.4 %psum.28 = f32[]{:T(128)} all-reduce(f32[]{:T(128)} %convert_reduce_fusion.5), channel_id=1, replica_groups=mesh['dp'=16,'seq'=2] {'dp','seq'}, use_global_device_ids=true, to_apply=%region_23.24 | all-reduce | flops 1 | bytes 8 | tf_op jit(solution)/shard_map/psum | solution.py:320
  59.7 5.8 sort.17
  67.6 2.7 multiply_sine_fusion.1
  70.2 135.1 %all-gather.5.cloned.1.call-done = bf16[10880,768]{1,0:T(8,128)(2,1)} async-done(((bf16[680,768]{1,0:T(8,128)(2,1)}), bf16[10880,768]{1,0:T(8,128)(2,1)}) %all-gather.5.cloned.1.call-update) | async-done | bytes 16711696 | tf_op jit(solution)/shard_map/all_gather | solution.py:307
  205.3 28.0 %reshape.817 = bf16[2720,4,768]{2,1,0:T(4,128)(2,1)} reshape(bf16[10880,768]{1,0:T(8,128)(2,1)} %all-gather.5.cloned.1.call-done) | data formatting | bytes 33423360 | tf_op jit(solution)/shard_map/reshape | solution.py:71
  233.4 26.2 %gather_fusion.1 = bf16[2720,4,768]{2,1,0:T(4,128)(2,1)} fusion(bf16[2720,4,768]{2,1,0:T(4,128)(2,1)} %reshape.817, s32[3072]{0:T(1024)S(1)} %pad_clamp_fusion.1), kind=kCustom, calls=%fused_computation.1 | custom fusion | bytes 33434240 | tf_op jit(solution)/shard_map/gather | solution.py:71
  259.6 26.7 %reshape.818 = bf16[10880,768]{1,0:T(8,128)(2,1)} reshape(bf16[2720,4,768]{2,1,0:T(4,128)(2,1)} %gather_fusion.1) | data formatting | bytes 33423360 | tf_op jit(solution)/shard_map/reshape | solution.py:71
  286.3 5.0 slice.238
  291.3 3.8 fusion.164
  295.2 102.2 %all-gather.3.cloned.1.call-done = bf16[10880,768]{1,0:T(8,128)(2,1)} async-done(((bf16[680,768]{1,0:T(8,128)(2,1)}), bf16[10880,768]{1,0:T(8,128)(2,1)}) %all-gather.3.cloned.1.call-update) | async-done | bytes 16711696 | tf_op jit(solution)/shard_map/all_gather | solution.py:306
  397.3 27.9 %reshape.812 = bf16[2720,4,768]{2,1,0:T(4,128)(2,1)} reshape(bf16[10880,768]{1,0:T(8,128)(2,1)} %all-gather.3.cloned.1.call-done) | data formatting | bytes 33423360 | tf_op jit(solution)/shard_map/reshape | solution.py:71
  425.2 26.4 %gather_fusion = bf16[2720,4,768]{2,1,0:T(4,128)(2,1)} fusion(bf16[2720,4,768]{2,1,0:T(4,128)(2,1)} %reshape.812, s32[3072]{0:T(1024)S(1)} %pad_clamp_fusion.1), kind=kCustom, calls=%fused_computation | custom fusion | bytes 33434240 | tf_op jit(solution)/shard_map/gather | solution.py:71
  451.6 5.0 slice.229
  456.7 26.6 %reshape.813 = bf16[10880,768]{1,0:T(8,128)(2,1)} reshape(bf16[2720,4,768]{2,1,0:T(4,128)(2,1)} %gather_fusion) | data formatting | bytes 33423360 | tf_op jit(solution)/shard_map/reshape | solution.py:71
  483.3 4.3 fusion.162
  487.6 10.6 fusion.163
  501.1 3.2 slice.176
  504.3 3.2 slice.204
  507.4 17.8 %reshape.819 = bf16[768,2304]{1,0:T(8,128)(2,1)} reshape(bf16[576,4,768]{2,1,0:T(4,128)(2,1)} %slice.238) | data formatting | bytes 7077888 | tf_op jit(solution)/shard_map/reshape | solution.py:57
  525.3 2.1 fusion.167
  528.3 2.2 convolution_convert_fusion
  530.5 2.4 copy.39
  532.8 3.5 reshape.820
  536.4 3.3 fusion.166
  539.6 7.2 reshape.815
  548.6 3.2 slice.166
  551.8 2.2 fusion.169
  554.8 2.2 convolution_convert_fusion.1
  557.0 2.4 copy.34
  559.4 3.5 reshape.816
  562.9 2.2 fusion.165
  567.6 8.5 slice.211
  576.1 5.5 copy.83
  584.5 10.5 fusion.161
  595.1 9.0 slice.193
  604.1 5.6 copy.81
  619.0 7.5 fusion.172
  633.5 4.7 convolution_add_fusion.1
  638.3 2.1 fusion.176
  644.5 3.8 convert_reduce_fusion
  648.2 2.2 multiply_reduce_fusion.4
  653.5 1.9 copy.49
  655.4 1.9 reshape.825
  659.6 1.9 fusion.64
  661.6 5.2 fusion.156
  666.9 2.1 fusion.157
  669.0 1.8 multiply_reduce_fusion.1
  679.1 11.8 reshape.841
  692.3 7.7 fusion.145
  707.0 4.2 fusion.42
  711.9 8.4 reshape.840
  720.3 2.0 convolution_bitcast_fusion
  722.5 78.6 %concatenate.9 = f32[10880,768]{1,0:T(8,128)} concatenate(f32[1,768]{1,0:T(1,128)S(1)} %reshape.826, f32[1,768]{1,0:T(1,128)S(1)} %reshape.827, f32[1,768]{1,0:T(1,128)S(1)} %reshape.828, f32[1,768]{1,0:T(1,128)S(1)} %reshape.829, f32[1,768]{1,0:T(1,128)S(1)} %reshape.830, f32[1,768]{1,0:T(1,128)S(1)} %copy-done.82, f32[1,768]{1,0:T(1,128)S(1)} %copy-done.83, ...), dimensions={0} | concatenate | bytes 66846720 | tf_op jit(solution)/shard_map/concatenate | solution.py:65
  801.1 37.8 %reshape.842 = f32[2720,4,768]{2,1,0:T(4,128)} reshape(f32[10880,768]{1,0:T(8,128)} %concatenate.9) | data formatting | bytes 66846720 | tf_op jit(solution)/shard_map/reshape | solution.py:71
  838.9 32.6 %gather_fusion.2 = f32[2720,4,768]{2,1,0:T(4,128)} fusion(f32[2720,4,768]{2,1,0:T(4,128)} %reshape.842, s32[3072]{0:T(1024)S(1)} %copy-done.60), kind=kCustom, calls=%fused_computation.2 | custom fusion | bytes 66857600 | tf_op jit(solution)/shard_map/gather | solution.py:71
  871.5 38.5 %reshape.843 = f32[10880,768]{1,0:T(8,128)} reshape(f32[2720,4,768]{2,1,0:T(4,128)} %gather_fusion.2) | data formatting | bytes 66846720 | tf_op jit(solution)/shard_map/reshape | solution.py:71
  910.1 494.6 %reduce-scatter.2.cloned.1.call-done = f32[680,768]{1,0:T(8,128)} async-done(((f32[10880,768]{1,0:T(8,128)}), f32[680,768]{1,0:T(8,128)}) %reduce-scatter.2.cloned.1.call-update) | async-done | bytes 2088976 | tf_op jit(solution)/shard_map/reduce_scatter | solution.py:383
  1406.3 21.3 %all-reduce.2.cloned.1.call-done = f32[680,768]{1,0:T(8,128)} async-done(((f32[680,768]{1,0:T(8,128)}), f32[680,768]{1,0:T(8,128)}) %all-reduce.2.cloned.1.call-update) | async-done | bytes 2088976 | tf_op jit(solution)/shard_map/psum | solution.py:384
  1427.6 2.7 multiply_reduce_fusion
  1430.3 40.5 %psum.29 = f32[]{:T(128)} all-reduce(f32[]{:T(128)S(6)} %mul.479), channel_id=1, replica_groups=mesh['dp'=16,'seq'=2] {'dp','seq'}, use_global_device_ids=true, to_apply=%region_24.25 | all-reduce | flops 1 | bytes 8 | tf_op jit(solution)/shard_map/psum | solution.py:361
  1470.8 41.3 %psum.31 = f32[]{:T(128)} all-reduce(f32[]{:T(128)} %multiply_reduce_fusion), channel_id=1, replica_groups=mesh['dp'=16,'seq'=2] {'dp'}, use_global_device_ids=true, to_apply=%region_49.50 | all-reduce | flops 1 | bytes 8 | tf_op jit(solution)/shard_map/psum | solution.py:385
  1512.9 6.9 fusion.158
  (347 shorter events, 58.3 us)
Async XLA Ops:
  7.2 518.1 %copy-start = (bf16[2,128,768]{2,1,0:T(8,128)(2,1)S(1)}, bf16[2,128,768]{2,1,0:T(8,128)(2,1)}, u32[]{:S(2)}) copy-start(bf16[2,128,768]{2,1,0:T(8,128)(2,1)} %param.9) | copy-start | bytes 1179652
  7.2 198.1 %all-gather.5.cloned.1.call-start = ((), (), s32[]{:S(2)}) async-start(), calls=%async_computation.2 | async-start | bytes 17756160 | tf_op jit(solution)/shard_map/all_gather | solution.py:307
  7.9 2.8 copy-start.108
  7.9 2.9 copy-start.1
  7.9 51.8 %copy-start.61 = (s32[2720]{0:T(1024)S(1)}, s32[2720]{0:T(1024)}, u32[]{:S(2)}) copy-start(s32[2720]{0:T(1024)} %param.12) | copy-start | bytes 32644
  7.9 389.4 %all-gather.3.cloned.1.call-start = ((), (), s32[]{:S(2)}) async-start(), calls=%async_computation.1 | async-start | bytes 17756160 | tf_op jit(solution)/shard_map/all_gather | solution.py:306
  10.7 1394.1 %reduce-scatter.2.cloned.1.call-start = ((), (), s32[]{:S(2)}) async-start(), calls=%async_computation.3 | async-start | bytes 35512320 | tf_op jit(solution)/shard_map/reduce_scatter | solution.py:383
  525.3 3.0 copy-start.30
  525.3 3.0 copy-start.94
  548.6 5.6 copy-start.54
  548.6 5.6 copy-start.58
  551.8 3.0 copy-start.28
  553.9 3.0 copy-start.66
  554.2 2.8 copy-start.70
  562.9 3.1 copy-start.36
  562.9 3.2 copy-start.42
  565.1 46.4 %copy-start.31 = (bf16[2,128,1,12,64]{1,0,4,3,2:T(2,128)(2,1)}, bf16[2,128,1,12,64]{1,0,4,3,2:T(2,128)(2,1)S(1)}, u32[]{:S(2)}) copy-start(bf16[2,128,1,12,64]{1,0,4,3,2:T(2,128)(2,1)S(1)} %get-tuple-element.74) | copy-start | bytes 1179652
  565.1 46.4 %copy-start.34 = (bf16[2,128,1,12,64]{1,0,4,3,2:T(2,128)(2,1)}, bf16[2,128,1,12,64]{1,0,4,3,2:T(2,128)(2,1)S(1)}, u32[]{:S(2)}) copy-start(bf16[2,128,1,12,64]{1,0,4,3,2:T(2,128)(2,1)S(1)} %get-tuple-element.76) | copy-start | bytes 1179652
  567.6 45.1 %collective-permute-start = (bf16[4,2,128,12,64]{2,4,3,1,0:T(8,128)(2,1)}, bf16[4,2,128,12,64]{2,4,3,1,0:T(8,128)(2,1)}, u32[]{:S(2)}, u32[]{:S(2)}) collective-permute-start(bf16[4,2,128,12,64]{2,4,3,1,0:T(8,128)(2,1)} %pad_maximum_fusion), channel_id=1, source_target_pairs={{0,1},{1,0},{2,3},{3,2},{4,5},{5,4},{6,7},{7,6},{8,9},{9,8},{10,11... | collective-permute-start | bytes 4718600 | tf_op jit(solution)/shard_map/ppermute | solution.py:26
  576.1 5.5 copy-start.62
  604.0 6.9 copy-start.43
  604.0 6.9 copy-start.49
  604.1 6.9 copy-start.106
  626.5 2.7 copy-start.79
  632.5 5.7 slice-start.2
  633.1 17.3 %copy-start.8 = (f32[256,768]{1,0:T(8,128)}, f32[256,768]{1,0:T(8,128)S(1)}, u32[]{:S(2)}) copy-start(f32[256,768]{1,0:T(8,128)S(1)} %get-tuple-element.114) | copy-start | bytes 2359300
  633.2 17.2 %copy-start.68 = (f32[256]{0:T(256)}, f32[256]{0:T(256)S(1)}, u32[]{:S(2)}) copy-start(f32[256]{0:T(256)S(1)} %broadcast_multiply_fusion.9) | copy-start | bytes 3076
  633.4 17.0 %copy-start.80 = (f32[256]{0:T(256)}, f32[256]{0:T(256)S(1)}, u32[]{:S(2)}) copy-start(f32[256]{0:T(256)S(1)} %add_rsqrt_fusion.3) | copy-start | bytes 3076
  633.5 4.8 slice-start.3
  633.5 4.8 copy-start.101
  638.2 6.2 copy-start.26
  638.3 2.6 copy-start.48
  638.3 2.6 copy-start.64
  638.3 2.6 copy-start.76
  640.4 3.1 copy-start.17
  640.4 3.1 copy-start.72
  640.6 2.9 copy-start.92
  643.5 4.7 slice-start
  644.4 6.0 copy-start.15
  644.4 3.8 slice-start.1
  661.6 5.3 copy-start.18
  661.6 5.3 copy-start.51
  661.6 5.3 copy-start.65
  661.6 5.2 copy-start.73
  661.6 5.2 copy-start.77
  661.6 5.2 copy-start.93
  671.5 2.7 copy-start.19
  671.5 2.7 copy-start.21
  672.4 3.1 copy-start.98
  672.4 3.7 copy-start.74
  672.4 4.2 copy-start.97
  672.4 4.8 copy-start.96
  672.5 5.4 copy-start.95
  672.5 6.0 copy-start.90
  673.4 26.6 %collective-permute-start.1 = (bf16[2,2,128,12,64]{2,4,3,1,0:T(8,128)(2,1)}, bf16[2,2,128,12,64]{2,4,3,1,0:T(8,128)(2,1)}, u32[]{:S(2)}, u32[]{:S(2)}) collective-permute-start(bf16[2,2,128,12,64]{2,4,3,1,0:T(8,128)(2,1)} %pad_maximum_fusion.2), channel_id=1, source_target_pairs={{0,1},{1,0},{2,3},{3,2},{4,5},{5,4},{6,7},{7,6},{8,9},{9,8},{10,11... | collective-permute-start | bytes 2359304 | tf_op jit(solution)/shard_map/ppermute | solution.py:26
  679.1 11.8 copy-start.20
  707.0 4.3 copy-start.7
  707.0 4.3 copy-start.103
  707.0 4.3 copy-start.104
  707.0 4.3 copy-start.109
  711.8 8.5 copy-start.102
  801.1 37.8 %copy-start.60 = (s32[3072]{0:T(1024)S(1)}, s32[3072]{0:T(1024)}, u32[]{:S(2)}) copy-start(s32[3072]{0:T(1024)} %pad_clamp_fusion) | copy-start | bytes 36868
  910.0 517.6 %all-reduce.2.cloned.1.call-start = ((), (), s32[]{:S(2)}) async-start(), calls=%async_computation.4 | async-start | bytes 4177920 | tf_op jit(solution)/shard_map/psum | solution.py:384
  1404.7 108.1 %copy-start.14 = (f32[680,768]{1,0:T(8,128)S(1)}, f32[680,768]{1,0:T(8,128)}, u32[]{:S(2)}) copy-start(f32[680,768]{1,0:T(8,128)} %param.13) | copy-start | bytes 6266884
  (56 other events, 98.3 us)
Sparse Core Ops, SparseCore 0:
  10.8 194.4 all-gather.4
  208.7 188.5 all-gather.2
  910.2 494.5 reduce-scatter.1
  1406.9 20.6 all-reduce.1
where the time goes:
time: 1550 us; the launch traced here: 1530 us
  waiting for transfers between devices  754 us (49%)
  local copies, waits for them, and re-layouts  512 us (33%)
  blocking collectives  126 us (8%)
  matrix products  74.8 us (5%)
  other arithmetic  40.3 us (3%)
  between operations  19.9 us (1%)
    reduce_scatter x1, waiting for transfers between devices, on_device(): lax.psum_scatter(stored_grad, 'dp', scatter_dimension=0, tiled=True)  495 us
    reshape x6, local copies, waits for them, and re-layouts, reorder(): return stored.reshape(order.shape[0], -1, D)[order].reshape(-1, D)  186 us
    all_gather x1, waiting for transfers between devices, on_device(): lax.all_gather(teacher, 'dp', axis=0, tiled=True)  135 us
    all_gather x1, waiting for transfers between devices, on_device(): lax.all_gather(weights.astype(jnp.bfloat16), 'dp', axis=0, tiled=True)  102 us
    gather x3, local copies, waits for them, and re-layouts, reorder(): return stored.reshape(order.shape[0], -1, D)[order].reshape(-1, D)  85.2 us
    concatenate x1, local copies, waits for them, and re-layouts, pack_flat(): jnp.concatenate([stacked, jnp.zeros((total_rows - stacked.shape[0], D), s...  78.6 us
    slice x13, local copies, waits for them, and re-layouts, unpack(): tables[entry_name] = flat[offset:offset + entry_rows].reshape(entry_shape)  68.6 us
    psum x1, blocking collectives, on_device(): lax.psum(jnp.sum(hidden_mask.astype(jnp.float32)), ('dp', 'seq'))  44.4 us
  transfers between devices with their start and end apart: 6, of which 4 were waited for; matrix products, arithmetic and copies ran while one was open for 12% of the time, Pallas kernels for 0%

commit v1 on v0

--- a/solution.py
+++ b/solution.py
@@ -20,6 +20,13 @@
 BETA_TWO = 0.999
 ADAM_EPS = 1e-08
 NORM_EPS = 1e-06
+
+
+def serve_routes_all(q_in, k_dim):
+    val = list(q_in.shape[1:])
+    val[k_dim] *= q_in.shape[0]
+    inter = jnp.moveaxis(q_in, 0, k_dim).reshape(val)
+    return inter
 
 
 def from_partner(shard, axis, bit):
@@ -302,9 +309,33 @@
     second_moment,
     step_count,
 ):
+
+    def solve_units(point, axis_name, d_out):
+        n_blocks = jax.lax.psum(1, axis_name)
+        heap = tuple(((b, (b + 1) % n_blocks) for b in range(n_blocks)))
+        parts_seen = tuple(((it, m) for m, it in heap))
+        field_out, main = ([], [])
+        num = 0
+        while num < n_blocks - 1:
+            if num % 2 == 0:
+                state_next = jax.lax.ppermute(
+                    field_out[-1] if field_out else point, axis_name, heap
+                )
+                field_out.append(state_next)
+            else:
+                long_array = jax.lax.ppermute(main[-1] if main else point, axis_name, parts_seen)
+                main.append(long_array)
+            num = num + 1
+        then = jnp.stack([*field_out[::-1], point, *main])
+        known = jax.lax.axis_index(axis_name)
+        later = known - len(field_out)
+        then = then[(jnp.arange(n_blocks) - later) % n_blocks]
+        b_now = serve_routes_all(then, d_out)
+        return b_now
+
     gathered, teacher_all = (
         lax.all_gather(weights.astype(jnp.bfloat16), "dp", axis=0, tiled=True),
-        lax.all_gather(teacher, "dp", axis=0, tiled=True),
+        solve_units(teacher, "dp", 0),
     )
     inverse_order = jnp.argsort(span_order)
     params = unpack(reorder(gathered, inverse_order))

time: 1550 us -> 1750 us (1.13)
  waiting for transfers between devices: 754 us -> 825 us
  starting transfers between devices: 0.66 us -> 63.7 us
  blocking collectives: 126 us -> 169 us
  local copies, waits for them, and re-layouts: 512 us -> 537 us
    ppermute x0 -> x15, waiting for transfers between devices: none -> 309 us  [the longest x8 261 us: solve_units(): jax.lax.ppermute(field_out[-1] if field_out else point, axis_name, heap)]
    all_gather x1 -> x0, waiting for transfers between devices: 135 us -> none  [on_device(): lax.all_gather(teacher, 'dp', axis=0, tiled=True)]
    all_gather x1, waiting for transfers between devices: 102 us -> 0.01 us  [on_device(): lax.all_gather(weights.astype(jnp.bfloat16), 'dp', axis=0, tiled=True)]
    ppermute x0 -> x15, starting transfers between devices: none -> 63.1 us  [the longest x8 46.7 us: solve_units(): jax.lax.ppermute(field_out[-1] if field_out else point, axis_name, heap)]
    psum x1, blocking collectives: 44.4 us -> 86.9 us  [on_device(): lax.psum(jnp.sum(hidden_mask.astype(jnp.float32)), ('dp', 'seq'))]
    another operation x0 -> x2, local copies, waits for them, and re-layouts: none -> 29 us  [the longest x1 27.9 us: reorder(): return stored.reshape(order.shape[0], -1, D)[order].reshape(-1, D)]
    unnamed x234 -> x283, local copies, waits for them, and re-layouts: 17.1 us -> 46 us
    reshape x6 -> x5, local copies, waits for them, and re-layouts: 186 us -> 158 us  [reorder(): return stored.reshape(order.shape[0], -1, D)[order].reshape(-1, D)]
  transfers between devices with their start and end apart: 6 -> 20, of which waited for: 4 -> 11; matrix products, arithmetic and copies ran while one was open for 12% -> 15% of each run, Pallas kernels for 0% -> 0%
where the time goes in v1:
time: 1750 us; the launch traced here: 1740 us
  waiting for transfers between devices  825 us (47%)
  local copies, waits for them, and re-layouts  537 us (31%)
  blocking collectives  169 us (10%)
  matrix products  74.3 us (4%)
  starting transfers between devices  63.7 us (4%)
  other arithmetic  49.5 us (3%)
  between operations  19.8 us (1%)
    reduce_scatter x1, waiting for transfers between devices, on_device(): lax.psum_scatter(stored_grad, 'dp', scatter_dimension=0, tiled=True)  494 us
    ppermute x8, waiting for transfers between devices, solve_units(): jax.lax.ppermute(field_out[-1] if field_out else point, axis_name, heap)  261 us
    reshape x5, local copies, waits for them, and re-layouts, reorder(): return stored.reshape(order.shape[0], -1, D)[order].reshape(-1, D)  158 us
    psum x1, blocking collectives, on_device(): lax.psum(jnp.sum(hidden_mask.astype(jnp.float32)), ('dp', 'seq'))  86.9 us
    gather x3, local copies, waits for them, and re-layouts, reorder(): return stored.reshape(order.shape[0], -1, D)[order].reshape(-1, D)  84.9 us
    concatenate x1, local copies, waits for them, and re-layouts, pack_flat(): jnp.concatenate([stacked, jnp.zeros((total_rows - stacked.shape[0], D), s...  78.6 us
    slice x13, local copies, waits for them, and re-layouts, unpack(): tables[entry_name] = flat[offset:offset + entry_rows].reshape(entry_shape)  67.5 us
    ppermute x7, waiting for transfers between devices, solve_units(): jax.lax.ppermute(main[-1] if main else point, axis_name, parts_seen)  48.8 us
  transfers between devices with their start and end apart: 20, of which 11 were waited for; matrix products, arithmetic and copies ran while one was open for 15% of the time, Pallas kernels for 0%

profile of v1, /device:TPU:0, one launch (start us, length us, event | category | flops | bytes accessed | tf_op | source)
XLA Modules:
  0.0 1737.9 jit_solution(12124418705771011849)
XLA Ops:
  7.3 2.7 convert_element_type.232
  10.1 3.0 collective-permute-start
  13.1 38.7 %collective-permute-done = bf16[680,768]{1,0:T(8,128)(2,1)S(1)} collective-permute-done((bf16[680,768]{1,0:T(8,128)(2,1)S(1)}, bf16[680,768]{1,0:T(8,128)(2,1)S(1)}, u32[]{:S(2)}, u32[]{:S(2)}) %collective-permute-start) | collective-permute-done | bytes 1044512 | tf_op jit(solution)/shard_map/ppermute | solution.py:321
  51.8 5.6 collective-permute-start.8
  57.4 81.8 %collective-permute-done.1 = bf16[680,768]{1,0:T(8,128)(2,1)S(1)} collective-permute-done((bf16[680,768]{1,0:T(8,128)(2,1)S(1)}, bf16[680,768]{1,0:T(8,128)(2,1)S(1)}, u32[]{:S(2)}, u32[]{:S(2)}) %collective-permute-start.1) | collective-permute-done | bytes 1044512 | tf_op jit(solution)/shard_map/ppermute | solution.py:321
  139.3 3.1 collective-permute-start.2
  142.4 2.5 collective-permute-start.9
  144.9 25.2 %collective-permute-done.2 = bf16[680,768]{1,0:T(8,128)(2,1)S(1)} collective-permute-done((bf16[680,768]{1,0:T(8,128)(2,1)S(1)}, bf16[680,768]{1,0:T(8,128)(2,1)S(1)}, u32[]{:S(2)}, u32[]{:S(2)}) %collective-permute-start.2) | collective-permute-done | bytes 1044512 | tf_op jit(solution)/shard_map/ppermute | solution.py:321
  170.1 24.5 %collective-permute-start.3 = (bf16[680,768]{1,0:T(8,128)(2,1)S(1)}, bf16[680,768]{1,0:T(8,128)(2,1)S(1)}, u32[]{:S(2)}, u32[]{:S(2)}) collective-permute-start(bf16[680,768]{1,0:T(8,128)(2,1)S(1)} %collective-permute-done.2), channel_id=1, source_target_pairs={{0,2},{2,4},{4,6},{6,8},{8,10},{10,12},{12,14},{14,16},{16,18},{18... | collective-permute-start | bytes 3133448 | tf_op jit(solution)/shard_map/ppermute | solution.py:321
  195.5 43.9 %collective-permute-done.3 = bf16[680,768]{1,0:T(8,128)(2,1)S(1)} collective-permute-done((bf16[680,768]{1,0:T(8,128)(2,1)S(1)}, bf16[680,768]{1,0:T(8,128)(2,1)S(1)}, u32[]{:S(2)}, u32[]{:S(2)}) %collective-permute-start.3) | collective-permute-done | bytes 1044512 | tf_op jit(solution)/shard_map/ppermute | solution.py:321
  241.9 30.6 %collective-permute-done.10 = bf16[680,768]{1,0:T(8,128)(2,1)} collective-permute-done((bf16[680,768]{1,0:T(8,128)(2,1)S(1)}, bf16[680,768]{1,0:T(8,128)(2,1)}, u32[]{:S(2)}, u32[]{:S(2)}) %collective-permute-start.10) | collective-permute-done | bytes 1044512 | tf_op jit(solution)/shard_map/ppermute | solution.py:326
  272.5 33.3 %collective-permute-done.4 = bf16[680,768]{1,0:T(8,128)(2,1)} collective-permute-done((bf16[680,768]{1,0:T(8,128)(2,1)S(1)}, bf16[680,768]{1,0:T(8,128)(2,1)}, u32[]{:S(2)}, u32[]{:S(2)}) %collective-permute-start.4) | collective-permute-done | bytes 1044512 | tf_op jit(solution)/shard_map/ppermute | solution.py:321
  305.8 2.6 collective-permute-start.5
  310.7 18.2 %collective-permute-done.11 = bf16[680,768]{1,0:T(8,128)(2,1)} collective-permute-done((bf16[680,768]{1,0:T(8,128)(2,1)}, bf16[680,768]{1,0:T(8,128)(2,1)}, u32[]{:S(2)}, u32[]{:S(2)}) %collective-permute-start.11) | collective-permute-done | bytes 1044512 | tf_op jit(solution)/shard_map/ppermute | solution.py:326
  328.8 34.8 %collective-permute-done.5 = bf16[680,768]{1,0:T(8,128)(2,1)} collective-permute-done((bf16[680,768]{1,0:T(8,128)(2,1)}, bf16[680,768]{1,0:T(8,128)(2,1)}, u32[]{:S(2)}, u32[]{:S(2)}) %collective-permute-start.5) | collective-permute-done | bytes 1044512 | tf_op jit(solution)/shard_map/ppermute | solution.py:321
  369.8 6.5 sort.17
  380.9 3.1 collective-permute-start.13
  384.0 2.9 collective-permute-done.6
  386.9 8.6 collective-permute-start.7
  395.5 86.9 %psum.28 = f32[]{:T(128)} all-reduce(f32[]{:T(128)} %convert_reduce_fusion.5), channel_id=1, replica_groups=mesh['dp'=16,'seq'=2] {'dp','seq'}, use_global_device_ids=true, to_apply=%region_23.24 | all-reduce | flops 1 | bytes 8 | tf_op jit(solution)/shard_map/psum | solution.py:351
  487.8 3.0 multiply_sine_fusion.1
  490.8 5.0 collective-permute-start.14
  522.7 13.0 gather_fusion.1
  535.7 27.9 %reshape_reshape.3 = bf16[2720,4,768]{2,1,0:T(4,128)(2,1)} reshape(bf16[16,680,768]{2,1,0:T(8,128)(2,1)} %gather_fusion.1) | data formatting | bytes 33423360 | tf_op jit(solution)/shard_map/reshape;reshape | solution.py:78
  563.6 26.2 %gather_fusion.2 = bf16[2720,4,768]{2,1,0:T(4,128)(2,1)} fusion(bf16[2720,4,768]{2,1,0:T(4,128)(2,1)} %reshape_reshape.3, s32[3072]{0:T(1024)S(1)} %pad_clamp_fusion.1), kind=kCustom, calls=%fused_computation.2 | custom fusion | bytes 33434240 | tf_op jit(solution)/shard_map/gather | solution.py:78
  589.7 26.7 %reshape.863 = bf16[10880,768]{1,0:T(8,128)(2,1)} reshape(bf16[2720,4,768]{2,1,0:T(4,128)(2,1)} %gather_fusion.2) | data formatting | bytes 33423360 | tf_op jit(solution)/shard_map/reshape | solution.py:78
  616.4 5.0 slice.240
  621.4 3.4 fusion.166
  625.2 7.3 reshape.864
  642.9 10.6 fusion.165
  653.4 27.9 %reshape.858 = bf16[2720,4,768]{2,1,0:T(4,128)(2,1)} reshape(bf16[10880,768]{1,0:T(8,128)(2,1)} %all-gather.2.cloned.1.call-done) | data formatting | bytes 33423360 | tf_op jit(solution)/shard_map/reshape | solution.py:78
  681.4 26.2 %gather_fusion = bf16[2720,4,768]{2,1,0:T(4,128)(2,1)} fusion(bf16[2720,4,768]{2,1,0:T(4,128)(2,1)} %reshape.858, s32[3072]{0:T(1024)S(1)} %pad_clamp_fusion.1), kind=kCustom, calls=%fused_computation | custom fusion | bytes 33434240 | tf_op jit(solution)/shard_map/gather | solution.py:78
  707.5 5.0 slice.231
  712.5 26.8 %reshape.859 = bf16[10880,768]{1,0:T(8,128)(2,1)} reshape(bf16[2720,4,768]{2,1,0:T(4,128)(2,1)} %gather_fusion) | data formatting | bytes 33423360 | tf_op jit(solution)/shard_map/reshape | solution.py:78
  739.3 4.6 fusion.164
  743.9 7.2 reshape.861
  752.9 3.2 slice.166
  763.9 3.5 reshape.862
  767.4 3.1 fusion.167
  773.5 3.2 slice.204
  776.6 8.5 slice.211
  785.2 5.5 copy.83
  790.7 3.2 slice.198
  795.0 10.5 fusion.163
  805.5 9.0 slice.193
  814.5 5.5 copy.81
  830.0 7.5 fusion.174
  844.5 4.5 convolution_add_fusion.1
  855.3 3.8 convert_reduce_fusion
  872.5 5.2 fusion.158
  889.9 11.8 reshape.886
  903.2 7.7 fusion.147
  917.9 4.2 fusion.42
  922.7 8.4 reshape.885
  933.3 78.6 %concatenate.9 = f32[10880,768]{1,0:T(8,128)} concatenate(f32[1,768]{1,0:T(1,128)S(1)} %reshape.871, f32[1,768]{1,0:T(1,128)S(1)} %reshape.872, f32[1,768]{1,0:T(1,128)S(1)} %reshape.873, f32[1,768]{1,0:T(1,128)S(1)} %reshape.874, f32[1,768]{1,0:T(1,128)S(1)} %reshape.875, f32[1,768]{1,0:T(1,128)S(1)} %copy-done.95, f32[1,768]{1,0:T(1,128)S(1)} %copy-done.96, ...), dimensions={0} | concatenate | bytes 66846720 | tf_op jit(solution)/shard_map/concatenate | solution.py:72
  1011.9 37.8 %reshape.887 = f32[2720,4,768]{2,1,0:T(4,128)} reshape(f32[10880,768]{1,0:T(8,128)} %concatenate.9) | data formatting | bytes 66846720 | tf_op jit(solution)/shard_map/reshape | solution.py:78
  1049.7 32.6 %gather_fusion.3 = f32[2720,4,768]{2,1,0:T(4,128)} fusion(f32[2720,4,768]{2,1,0:T(4,128)} %reshape.887, s32[3072]{0:T(1024)S(1)} %copy-done.73), kind=kCustom, calls=%fused_computation.3 | custom fusion | bytes 66857600 | tf_op jit(solution)/shard_map/gather | solution.py:78
  1082.3 38.5 %reshape.888 = f32[10880,768]{1,0:T(8,128)} reshape(f32[2720,4,768]{2,1,0:T(4,128)} %gather_fusion.3) | data formatting | bytes 66846720 | tf_op jit(solution)/shard_map/reshape | solution.py:78
  1120.9 494.0 %reduce-scatter.2.cloned.1.call-done = f32[680,768]{1,0:T(8,128)} async-done(((f32[10880,768]{1,0:T(8,128)}), f32[680,768]{1,0:T(8,128)}) %reduce-scatter.2.cloned.1.call-update) | async-done | bytes 2088976 | tf_op jit(solution)/shard_map/reduce_scatter | solution.py:414
  1616.4 21.5 %all-reduce.2.cloned.1.call-done = f32[680,768]{1,0:T(8,128)} async-done(((f32[680,768]{1,0:T(8,128)}), f32[680,768]{1,0:T(8,128)}) %all-reduce.2.cloned.1.call-update) | async-done | bytes 2088976 | tf_op jit(solution)/shard_map/psum | solution.py:415
  1637.9 2.7 multiply_reduce_fusion
  1640.6 40.4 %psum.29 = f32[]{:T(128)} all-reduce(f32[]{:T(128)S(6)} %mul.479), channel_id=1, replica_groups=mesh['dp'=16,'seq'=2] {'dp','seq'}, use_global_device_ids=true, to_apply=%region_24.25 | all-reduce | flops 1 | bytes 8 | tf_op jit(solution)/shard_map/psum | solution.py:392
  1681.1 41.3 %psum.31 = f32[]{:T(128)} all-reduce(f32[]{:T(128)} %multiply_reduce_fusion), channel_id=1, replica_groups=mesh['dp'=16,'seq'=2] {'dp'}, use_global_device_ids=true, to_apply=%region_49.50 | all-reduce | flops 1 | bytes 8 | tf_op jit(solution)/shard_map/psum | solution.py:416
  1723.1 6.9 fusion.160
  (427 shorter events, 131.1 us)
Async XLA Ops:
  7.2 627.0 %copy-start = (bf16[2,128,768]{2,1,0:T(8,128)(2,1)S(1)}, bf16[2,128,768]{2,1,0:T(8,128)(2,1)}, u32[]{:S(2)}) copy-start(bf16[2,128,768]{2,1,0:T(8,128)(2,1)} %param.9) | copy-start | bytes 1179652
  7.2 302.3 %copy-start.123 = (s32[2]{0:T(128)S(1)}, s32[2]{0:T(128)}, u32[]{:S(2)}) copy-start(s32[2]{0:T(128)} %param.11) | copy-start | bytes 28
  7.2 359.5 %copy-start.1 = (s32[2,196]{1,0:T(2,128)S(1)}, s32[2,196]{1,0:T(2,128)}, u32[]{:S(2)}) copy-start(s32[2,196]{1,0:T(2,128)} %param.10) | copy-start | bytes 4708
  7.2 362.6 %copy-start.74 = (s32[2720]{0:T(1024)S(1)}, s32[2720]{0:T(1024)}, u32[]{:S(2)}) copy-start(s32[2720]{0:T(1024)} %param.12) | copy-start | bytes 32644
  7.2 646.2 %all-gather.2.cloned.1.call-start = ((), (), s32[]{:S(2)}) async-start(), calls=%async_computation.1 | async-start | bytes 17756160 | tf_op jit(solution)/shard_map/all_gather | solution.py:337
  10.0 1604.8 %reduce-scatter.2.cloned.1.call-start = ((), (), s32[]{:S(2)}) async-start(), calls=%async_computation.2 | async-start | bytes 35512320 | tf_op jit(solution)/shard_map/reduce_scatter | solution.py:414
  10.1 41.7 %collective-permute-start = (bf16[680,768]{1,0:T(8,128)(2,1)S(1)}, bf16[680,768]{1,0:T(8,128)(2,1)S(1)}, u32[]{:S(2)}, u32[]{:S(2)}) collective-permute-start(bf16[680,768]{1,0:T(8,128)(2,1)S(1)} %copy-done.46), channel_id=1, source_target_pairs={{0,2},{2,4},{4,6},{6,8},{8,10},{10,12},{12,14},{14,16},{16,18},{18... | collective-permute-start | bytes 3133448 | tf_op jit(solution)/shard_map/ppermute | solution.py:321
  51.8 87.5 %collective-permute-start.1 = (bf16[680,768]{1,0:T(8,128)(2,1)S(1)}, bf16[680,768]{1,0:T(8,128)(2,1)S(1)}, u32[]{:S(2)}, u32[]{:S(2)}) collective-permute-start(bf16[680,768]{1,0:T(8,128)(2,1)S(1)} %collective-permute-done), channel_id=1, source_target_pairs={{0,2},{2,4},{4,6},{6,8},{8,10},{10,12},{12,14},{14,16},{16,18},{18... | collective-permute-start | bytes 3133448 | tf_op jit(solution)/shard_map/ppermute | solution.py:321
  51.8 90.5 %collective-permute-start.8 = (bf16[680,768]{1,0:T(8,128)(2,1)S(1)}, bf16[680,768]{1,0:T(8,128)(2,1)S(1)}, u32[]{:S(2)}, u32[]{:S(2)}) collective-permute-start(bf16[680,768]{1,0:T(8,128)(2,1)S(1)} %copy-done.46), channel_id=1, source_target_pairs={{2,0},{4,2},{6,4},{8,6},{10,8},{12,10},{14,12},{16,14},{18,16},{20... | collective-permute-start | bytes 3133448 | tf_op jit(solution)/shard_map/ppermute | solution.py:326
  139.3 55.3 %copy-start.47 = (bf16[680,768]{1,0:T(8,128)(2,1)}, bf16[680,768]{1,0:T(8,128)(2,1)S(1)}, u32[]{:S(2)}) copy-start(bf16[680,768]{1,0:T(8,128)(2,1)S(1)} %collective-permute-done.1) | copy-start | bytes 3133444
  139.3 30.8 %collective-permute-start.2 = (bf16[680,768]{1,0:T(8,128)(2,1)S(1)}, bf16[680,768]{1,0:T(8,128)(2,1)S(1)}, u32[]{:S(2)}, u32[]{:S(2)}) collective-permute-start(bf16[680,768]{1,0:T(8,128)(2,1)S(1)} %collective-permute-done.1), channel_id=1, source_target_pairs={{0,2},{2,4},{4,6},{6,8},{8,10},{10,12},{12,14},{14,16},{16,18},{18... | collective-permute-start | bytes 3133448 | tf_op jit(solution)/shard_map/ppermute | solution.py:321
  142.4 52.2 %collective-permute-start.9 = (bf16[680,768]{1,0:T(8,128)(2,1)S(1)}, bf16[680,768]{1,0:T(8,128)(2,1)S(1)}, u32[]{:S(2)}, u32[]{:S(2)}) collective-permute-start(bf16[680,768]{1,0:T(8,128)(2,1)S(1)} %collective-permute-done.8), channel_id=1, source_target_pairs={{2,0},{4,2},{6,4},{8,6},{10,8},{12,10},{14,12},{16,14},{18,16},{20... | collective-permute-start | bytes 3133448 | tf_op jit(solution)/shard_map/ppermute | solution.py:326
  170.1 102.4 %copy-start.51 = (bf16[680,768]{1,0:T(8,128)(2,1)}, bf16[680,768]{1,0:T(8,128)(2,1)S(1)}, u32[]{:S(2)}) copy-start(bf16[680,768]{1,0:T(8,128)(2,1)S(1)} %collective-permute-done.2) | copy-start | bytes 3133444
  170.1 69.4 %collective-permute-start.3 = (bf16[680,768]{1,0:T(8,128)(2,1)S(1)}, bf16[680,768]{1,0:T(8,128)(2,1)S(1)}, u32[]{:S(2)}, u32[]{:S(2)}) collective-permute-start(bf16[680,768]{1,0:T(8,128)(2,1)S(1)} %collective-permute-done.2), channel_id=1, source_target_pairs={{0,2},{2,4},{4,6},{6,8},{8,10},{10,12},{12,14},{14,16},{16,18},{18... | collective-permute-start | bytes 3133448 | tf_op jit(solution)/shard_map/ppermute | solution.py:321
  194.6 78.0 %collective-permute-start.10 = (bf16[680,768]{1,0:T(8,128)(2,1)S(1)}, bf16[680,768]{1,0:T(8,128)(2,1)}, u32[]{:S(2)}, u32[]{:S(2)}) collective-permute-start(bf16[680,768]{1,0:T(8,128)(2,1)S(1)} %collective-permute-done.9), channel_id=1, source_target_pairs={{2,0},{4,2},{6,4},{8,6},{10,8},{12,10},{14,12},{16,14},{18,16},{20... | collective-permute-start | bytes 3133448 | tf_op jit(solution)/shard_map/ppermute | solution.py:326
  239.4 33.1 %copy-start.53 = (bf16[680,768]{1,0:T(8,128)(2,1)}, bf16[680,768]{1,0:T(8,128)(2,1)S(1)}, u32[]{:S(2)}) copy-start(bf16[680,768]{1,0:T(8,128)(2,1)S(1)} %collective-permute-done.3) | copy-start | bytes 3133444
  239.4 66.4 %collective-permute-start.4 = (bf16[680,768]{1,0:T(8,128)(2,1)S(1)}, bf16[680,768]{1,0:T(8,128)(2,1)}, u32[]{:S(2)}, u32[]{:S(2)}) collective-permute-start(bf16[680,768]{1,0:T(8,128)(2,1)S(1)} %collective-permute-done.3), channel_id=1, source_target_pairs={{0,2},{2,4},{4,6},{6,8},{8,10},{10,12},{12,14},{14,16},{16,18},{18... | collective-permute-start | bytes 3133448 | tf_op jit(solution)/shard_map/ppermute | solution.py:321
  272.5 56.3 %collective-permute-start.11 = (bf16[680,768]{1,0:T(8,128)(2,1)}, bf16[680,768]{1,0:T(8,128)(2,1)}, u32[]{:S(2)}, u32[]{:S(2)}) collective-permute-start(bf16[680,768]{1,0:T(8,128)(2,1)} %collective-permute-done.10), channel_id=1, source_target_pairs={{2,0},{4,2},{6,4},{8,6},{10,8},{12,10},{14,12},{16,14},{18,16},{20... | collective-permute-start | bytes 3133448 | tf_op jit(solution)/shard_map/ppermute | solution.py:326
  305.8 57.8 %collective-permute-start.5 = (bf16[680,768]{1,0:T(8,128)(2,1)}, bf16[680,768]{1,0:T(8,128)(2,1)}, u32[]{:S(2)}, u32[]{:S(2)}) collective-permute-start(bf16[680,768]{1,0:T(8,128)(2,1)} %collective-permute-done.4), channel_id=1, source_target_pairs={{0,2},{2,4},{4,6},{6,8},{8,10},{10,12},{12,14},{14,16},{16,18},{18... | collective-permute-start | bytes 3133448 | tf_op jit(solution)/shard_map/ppermute | solution.py:321
  309.5 69.4 %copy-start.106 = (pred[128]{0:T(512)(128)(4,1)}, pred[128]{0:T(512)(128)(4,1)S(1)}, u32[]{:S(2)}) copy-start(pred[128]{0:T(512)(128)(4,1)S(1)} %get-tuple-element.126) | copy-start | bytes 388
  310.6 55.5 %copy-start.107 = (s32[2]{0:T(128)}, s32[2]{0:T(128)S(1)}, u32[]{:S(2)}) copy-start(s32[2]{0:T(128)S(1)} %get-tuple-element.93) | copy-start | bytes 28
  328.8 52.0 %collective-permute-start.12 = (bf16[680,768]{1,0:T(8,128)(2,1)}, bf16[680,768]{1,0:T(8,128)(2,1)}, u32[]{:S(2)}, u32[]{:S(2)}) collective-permute-start(bf16[680,768]{1,0:T(8,128)(2,1)} %collective-permute-done.11), channel_id=1, source_target_pairs={{2,0},{4,2},{6,4},{8,6},{10,8},{12,10},{14,12},{16,14},{18,16},{20... | collective-permute-start | bytes 3133448 | tf_op jit(solution)/shard_map/ppermute | solution.py:326
  363.7 23.2 %collective-permute-start.6 = (bf16[680,768]{1,0:T(8,128)(2,1)}, bf16[680,768]{1,0:T(8,128)(2,1)}, u32[]{:S(2)}, u32[]{:S(2)}) collective-permute-start(bf16[680,768]{1,0:T(8,128)(2,1)} %collective-permute-done.5), channel_id=1, source_target_pairs={{0,2},{2,4},{4,6},{6,8},{8,10},{10,12},{12,14},{14,16},{16,18},{18... | collective-permute-start | bytes 3133448 | tf_op jit(solution)/shard_map/ppermute | solution.py:321
  380.9 109.9 %collective-permute-start.13 = (bf16[680,768]{1,0:T(8,128)(2,1)}, bf16[680,768]{1,0:T(8,128)(2,1)}, u32[]{:S(2)}, u32[]{:S(2)}) collective-permute-start(bf16[680,768]{1,0:T(8,128)(2,1)} %collective-permute-done.12), channel_id=1, source_target_pairs={{2,0},{4,2},{6,4},{8,6},{10,8},{12,10},{14,12},{16,14},{18,16},{20... | collective-permute-start | bytes 3133448 | tf_op jit(solution)/shard_map/ppermute | solution.py:326
  386.9 108.9 %collective-permute-start.7 = (bf16[680,768]{1,0:T(8,128)(2,1)}, bf16[680,768]{1,0:T(8,128)(2,1)}, u32[]{:S(2)}, u32[]{:S(2)}) collective-permute-start(bf16[680,768]{1,0:T(8,128)(2,1)} %collective-permute-done.6), channel_id=1, source_target_pairs={{0,2},{2,4},{4,6},{6,8},{8,10},{10,12},{12,14},{14,16},{16,18},{18... | collective-permute-start | bytes 3133448 | tf_op jit(solution)/shard_map/ppermute | solution.py:321
  490.8 30.8 %collective-permute-start.14 = (bf16[680,768]{1,0:T(8,128)(2,1)}, bf16[680,768]{1,0:T(8,128)(2,1)S(1)}, u32[]{:S(2)}, u32[]{:S(2)}) collective-permute-start(bf16[680,768]{1,0:T(8,128)(2,1)} %collective-permute-done.13), channel_id=1, source_target_pairs={{2,0},{4,2},{6,4},{8,6},{10,8},{12,10},{14,12},{16,14},{18,16},{20... | collective-permute-start | bytes 3133448 | tf_op jit(solution)/shard_map/ppermute | solution.py:326
  500.4 4.7 copy-start.54
  625.2 9.0 copy-start.60
  625.2 9.0 copy-start.62
  625.2 9.0 copy-start.63
  625.2 9.0 copy-start.64
  625.2 9.0 copy-start.121
  625.2 9.0 copy-start.124
  751.2 4.9 copy-start.61
  751.2 4.9 copy-start.117
  751.2 4.9 copy-start.122
  751.2 4.9 copy-start.125
  752.9 5.8 copy-start.67
  752.9 5.8 copy-start.71
  772.8 50.8 %collective-permute-start.15 = (bf16[4,2,128,12,64]{2,4,3,1,0:T(8,128)(2,1)}, bf16[4,2,128,12,64]{2,4,3,1,0:T(8,128)(2,1)}, u32[]{:S(2)}, u32[]{:S(2)}) collective-permute-start(bf16[4,2,128,12,64]{2,4,3,1,0:T(8,128)(2,1)} %pad_maximum_fusion), channel_id=1, source_target_pairs={{0,1},{1,0},{2,3},{3,2},{4,5},{5,4},{6,7},{7,6},{8,9},{9,8},{10,11... | collective-permute-start | bytes 4718600 | tf_op jit(solution)/shard_map/ppermute | solution.py:33
  843.6 5.5 slice-start.2
  844.2 17.1 copy-start.8
  844.2 17.1 copy-start.80
  844.4 16.9 copy-start.93
  844.5 4.6 slice-start.3
  844.5 4.6 copy-start.114
  849.1 6.3 copy-start.26
  854.4 4.7 slice-start
  855.3 6.0 copy-start.15
  872.4 5.3 copy-start.18
  872.4 5.3 copy-start.59
  872.4 5.3 copy-start.77
  872.4 5.2 copy-start.85
  872.4 5.2 copy-start.89
  872.5 5.2 copy-start.105
  883.3 4.8 copy-start.109
  883.3 5.4 copy-start.108
  883.3 6.0 copy-start.103
  884.3 26.7 %collective-permute-start.16 = (bf16[2,2,128,12,64]{2,4,3,1,0:T(8,128)(2,1)}, bf16[2,2,128,12,64]{2,4,3,1,0:T(8,128)(2,1)}, u32[]{:S(2)}, u32[]{:S(2)}) collective-permute-start(bf16[2,2,128,12,64]{2,4,3,1,0:T(8,128)(2,1)} %pad_maximum_fusion.2), channel_id=1, source_target_pairs={{0,1},{1,0},{2,3},{3,2},{4,5},{5,4},{6,7},{7,6},{8,9},{9,8},{10,11... | collective-permute-start | bytes 2359304 | tf_op jit(solution)/shard_map/ppermute | solution.py:33
  889.9 11.8 copy-start.20
  922.7 8.5 copy-start.115
  1011.9 37.8 %copy-start.73 = (s32[3072]{0:T(1024)S(1)}, s32[3072]{0:T(1024)}, u32[]{:S(2)}) copy-start(s32[3072]{0:T(1024)} %pad_clamp_fusion) | copy-start | bytes 36868
  1120.8 517.0 %all-reduce.2.cloned.1.call-start = ((), (), s32[]{:S(2)}) async-start(), calls=%async_computation.3 | async-start | bytes 4177920 | tf_op jit(solution)/shard_map/psum | solution.py:415
  1614.9 108.2 %copy-start.14 = (f32[680,768]{1,0:T(8,128)S(1)}, f32[680,768]{1,0:T(8,128)}, u32[]{:S(2)}) copy-start(f32[680,768]{1,0:T(8,128)} %param.13) | copy-start | bytes 6266884
  (87 other events, 194.8 us)
Sparse Core Ops, SparseCore 0:
  10.8 342.0 all-gather.1
  1121.0 493.8 reduce-scatter.1
  1617.2 20.6 all-reduce.1
